TPU v7x, 32 devices: a whole 2x2x4 slice. The times are simulated.
32 devices in a mesh: dp: 2 (over y), expert: 4 (over z), ffn: 4 (over x, core).
Axes of the slice: x: 2, y: 2, z: 4, core: 2. Of those that a mesh axis runs over, the one named last changes fastest.
Arguments:
- tokens: bfloat16 [512, 4096], P('expert'), may hold values from -6 to 6
- expert_ids: int32 [512, 2], P('expert'), may hold values from 0 to 3, all different within a row; in each aligned block of 128 rows (0 to 127, 128 to 255, ...) at most 64 rows name the same one
- route_weight: float32 [512, 2], P('expert'), may hold values from 0.05 to 1
- cotangent: bfloat16 [512, 4096], P('expert'), may hold values from -40 to 40
- w_gate: bfloat16 [4, 7168, 4096], P('expert', ('dp', 'ffn')), may hold values from -0.09375 to 0.09375
- w_up: bfloat16 [4, 7168, 4096], P('expert', ('dp', 'ffn')), may hold values from -0.09375 to 0.09375
- w_down: bfloat16 [4, 7168, 4096], P('expert', ('dp', 'ffn')), may hold values from -0.0625 to 0.0625
Outputs:
- layer_out: bfloat16 [512, 4096], P('expert', ('dp', 'ffn'))
- ascent_gate: bfloat16 [4, 7168, 4096], P('expert', ('dp', 'ffn'))
- ascent_up: bfloat16 [4, 7168, 4096], P('expert', ('dp', 'ffn'))
- ascent_down: bfloat16 [4, 7168, 4096], P('expert', ('dp', 'ffn'))
Inputs may be any that keep to these rules, and one draw needn't show every extreme that they name: `expert_ids`: each row names two different experts. Among the rows of one aligned block of 128 no expert is named more than 64 times; in every draw some block names some expert exactly 64 times.
All inputs are finite; a program needn't handle non-finite values.
Results may differ from a plain program's by a relative error of at most 0.017.
Values may be sent and summed in bfloat16 or wider, within the bound.
A program may use at most 128 MiB of HBM per device.

v0:
```python
import jax
import jax.numpy as jnp
from jax import lax
from jax.sharding import PartitionSpec as P

FF = 7168


def silu_parts(pre_act):
    sigmoid_value = jax.nn.sigmoid(pre_act)
    return (pre_act * sigmoid_value, sigmoid_value * (1.0 + pre_act * (1.0 - sigmoid_value)))


def against_rows(left_rows, right_rows):
    return lax.dot_general(
        left_rows, right_rows, (((0,), (0,)), ((), ())), preferred_element_type=jnp.float32
    )


def across_width(left_rows, weight):
    return lax.dot_general(
        left_rows, weight, (((1,), (1,)), ((), ())), preferred_element_type=jnp.float32
    )


def squares_of(matrix):
    return jnp.sum(matrix * matrix)


def on_device(tokens, expert_ids, route_weight, cotangent, w_gate, w_up, w_down):
    tok_rows, feature_width = tokens.shape
    experts = lax.axis_size("expert")
    groups = lax.axis_size(("dp", "ffn"))
    capacity = tok_rows // 2
    slot_count = experts * capacity
    column_width = feature_width // groups
    chosen = expert_ids[:, :, None] == jnp.arange(experts, dtype=jnp.int32)[None, None, :]
    per_token = jnp.sum(chosen.astype(jnp.int32), axis=1)
    earlier = jnp.cumsum(per_token, axis=0) - per_token
    position = jnp.sum(jnp.where(chosen, earlier[:, None, :], 0), axis=2)
    slot_index = expert_ids * capacity + position
    slot_hot = slot_index[:, :, None] == jnp.arange(slot_count, dtype=jnp.int32)[None, None, :]
    hot_all = slot_hot.reshape(tok_rows * 2, slot_count).astype(jnp.bfloat16)
    scaled = (route_weight[:, :, None] * cotangent.astype(jnp.float32)[:, None, :]).astype(
        jnp.bfloat16
    )
    token_slots = against_rows(hot_all, jnp.repeat(tokens, 2, axis=0)).astype(jnp.bfloat16)
    grad_slots = against_rows(hot_all, scaled.reshape(tok_rows * 2, feature_width)).astype(
        jnp.bfloat16
    )
    token_cube = token_slots.reshape(experts, capacity, feature_width)
    grad_cube = grad_slots.reshape(experts, capacity, feature_width)
    column_start = lax.axis_index(("dp", "ffn")) * column_width
    token_part = lax.dynamic_slice_in_dim(token_cube, column_start, column_width, 2)
    grad_part = lax.dynamic_slice_in_dim(grad_cube, column_start, column_width, 2)
    received = (
        lax.all_to_all(token_part, "expert", split_axis=0, concat_axis=0, tiled=True),
        lax.all_to_all(grad_part, "expert", split_axis=0, concat_axis=0, tiled=True),
    )
    slot_rows, slot_grads = (
        lax.all_gather(
            received[0].reshape(slot_count, column_width), ("dp", "ffn"), axis=1, tiled=True
        ),
        lax.all_gather(
            received[1].reshape(slot_count, column_width), ("dp", "ffn"), axis=1, tiled=True
        ),
    )
    gate_weight = w_gate[0]
    up_weight = w_up[0]
    down_weight = w_down[0]
    pre_gate = across_width(slot_rows, gate_weight)
    pre_up = across_width(slot_rows, up_weight)
    activated, derivative = silu_parts(pre_gate)
    hidden = (activated * pre_up).astype(jnp.bfloat16)
    partial_value = jnp.dot(hidden, down_weight, preferred_element_type=jnp.float32)
    grad_down = against_rows(hidden, slot_grads)
    grad_hidden = across_width(slot_grads, down_weight)
    delta_gate = (grad_hidden * pre_up * derivative).astype(jnp.bfloat16)
    delta_up = (grad_hidden * activated).astype(jnp.bfloat16)
    grad_gate = against_rows(delta_gate, slot_rows)
    grad_up = against_rows(delta_up, slot_rows)
    sum_squares = lax.psum(
        squares_of(grad_gate) + squares_of(grad_up) + squares_of(grad_down), ("dp", "expert", "ffn")
    )
    summed = lax.psum_scatter(
        partial_value.astype(jnp.bfloat16), ("dp", "ffn"), scatter_dimension=1, tiled=True
    )
    summed = summed.reshape(experts, capacity, column_width)
    returned_rows = lax.all_to_all(
        summed, "expert", split_axis=0, concat_axis=0, tiled=True
    ).reshape(slot_count, column_width)
    picked = jnp.dot(hot_all, returned_rows, preferred_element_type=jnp.float32).reshape(
        tok_rows, 2, column_width
    )
    layer_out = jnp.sum(route_weight[:, :, None] * picked, axis=1).astype(jnp.bfloat16)
    inv_rms = lax.rsqrt(sum_squares / (3.0 * experts * FF * feature_width) + 1e-06)
    return (
        layer_out,
        (grad_gate * inv_rms).astype(jnp.bfloat16)[None],
        (grad_up * inv_rms).astype(jnp.bfloat16)[None],
        (grad_down * inv_rms).astype(jnp.bfloat16)[None],
    )


def solution(mesh):
    return jax.shard_map(
        on_device,
        mesh=mesh,
        in_specs=(
            P("expert", None),
            P("expert", None),
            P("expert", None),
            P("expert", None),
            P("expert", ("dp", "ffn"), None),
            P("expert", ("dp", "ffn"), None),
            P("expert", ("dp", "ffn"), None),
        ),
        out_specs=(
            P("expert", ("dp", "ffn")),
            P("expert", ("dp", "ffn"), None),
            P("expert", ("dp", "ffn"), None),
            P("expert", ("dp", "ffn"), None),
        ),
        check_vma=False,
    )
```

profile of v0, /device:TPU:0, one launch (start us, length us, event | category | flops | bytes accessed | tf_op | source)
XLA Modules:
  0.0 195.2 jit_solution(6774078264472581371)
XLA Ops:
  7.2 0.0 all-gather.3.cloned.1.call-start
  7.3 0.8 convert_reduce_fusion
  8.1 0.1 copy.12
  8.2 0.2 reduce_window_sum.11
  8.4 0.1 copy.14
  8.4 0.7 select_reduce_fusion
  9.2 0.7 multiply_add_fusion
  9.8 0.7 fusion.14
  10.6 15.1 %all_to_all.15 = bf16[4,64,512]{2,1,0:T(8,128)(2,1)} all-to-all(bf16[4,64,512]{2,1,0:T(8,128)(2,1)S(1)} %constant_dynamic-slice_fusion), channel_id=1, replica_groups=mesh['dp'=2,'expert'=4,'ffn'=4] {'expert'}, dimensions={0} | all-to-all | bytes 524288 | tf_op jit(solution)/shard_map/all_to_all | solution.py:57
  25.7 0.0 all-gather.3.cloned.1.call-update
  25.8 0.0 all-gather.5.cloned.1.call-start
  25.8 0.2 convert_element_type.45
  26.0 0.8 fusion.15
  26.9 11.1 %all_to_all.16 = bf16[4,64,512]{2,1,0:T(8,128)(2,1)} all-to-all(bf16[4,64,512]{2,1,0:T(8,128)(2,1)S(1)} %constant_dynamic-slice_fusion.1), channel_id=1, replica_groups=mesh['dp'=2,'expert'=4,'ffn'=4] {'expert'}, dimensions={0} | all-to-all | bytes 524288 | tf_op jit(solution)/shard_map/all_to_all | solution.py:58
  38.0 0.0 all-gather.5.cloned.1.call-update
  38.0 0.2 reduce-scatter.2.cloned.1.call-start
  38.3 14.9 %all-gather.3.cloned.1.call-done = bf16[256,4096]{1,0:T(8,128)(2,1)} async-done(((bf16[256,512]{1,0:T(8,128)(2,1)}), bf16[256,4096]{1,0:T(8,128)(2,1)}) %all-gather.3.cloned.1.call-update) | async-done | bytes 2097168 | tf_op jit(solution)/shard_map/all_gather | solution.py:61
  53.1 6.2 %fusion.9 = f32[256,896]{1,0:T(8,128)S(1)} fusion(bf16[256,4096]{1,0:T(8,128)(2,1)} %all-gather.3.cloned.1.call-done, bf16[1,896,4096]{2,1,0:T(8,128)(2,1)} %param.11), kind=kOutput, calls=%fused_computation.15 | convolution fusion | flops 1879048192 | bytes 10354688 | tf_op jit(solution)/shard_map/dot_general | solution.py:21
  59.4 6.7 %multiply_convert_fusion.7 = (bf16[256,896]{1,0:T(8,128)(2,1)S(1)}, f32[256,896]{1,0:T(8,128)}) fusion(f32[256,896]{1,0:T(8,128)S(1)} %fusion.9, bf16[256,4096]{1,0:T(8,128)(2,1)S(1)} %copy-done.2, bf16[1,896,4096]{2,1,0:T(8,128)(2,1)} %param.12), kind=kOutput, calls=%fused_computation.30 | convolution fusion | flops 1880424448 | bytes 11730944 | tf_op jit(solution)/shard_map/dot_general | solution.py:21
  66.1 0.8 copy-done.5
  66.9 3.7 %fusion.11 = bf16[256,4096]{1,0:T(8,128)(2,1)} fusion(bf16[256,896]{1,0:T(8,128)(2,1)S(1)} %get-tuple-element.4, bf16[1,896,4096]{2,1,0:T(8,128)(2,1)S(1)} %bitcast.56), kind=kOutput, calls=%fused_computation.19 | convolution fusion | flops 1880096768 | bytes 9895936 | tf_op jit(solution)/shard_map/dot_general | solution.py:75
  70.5 0.0 reduce-scatter.2.cloned.1.call-update
  70.5 12.6 %all-gather.5.cloned.1.call-done = bf16[256,4096]{1,0:T(8,128)(2,1)} async-done(((bf16[256,512]{1,0:T(8,128)(2,1)}), bf16[256,4096]{1,0:T(8,128)(2,1)}) %all-gather.5.cloned.1.call-update) | async-done | bytes 2097168 | tf_op jit(solution)/shard_map/all_gather | solution.py:64
  83.1 6.1 %fusion.3 = f32[256,896]{1,0:T(8,128)S(1)} fusion(bf16[256,4096]{1,0:T(8,128)(2,1)} %all-gather.5.cloned.1.call-done, bf16[1,896,4096]{2,1,0:T(8,128)(2,1)} %param.13), kind=kOutput, calls=%fused_computation.9 | convolution fusion | flops 1879048192 | bytes 10354688 | tf_op jit(solution)/shard_map/dot_general | solution.py:21
  89.3 8.6 %multiply_reduce_fusion.2 = (f32[]{:T(128)}, f32[896,4096]{1,0:T(8,128)}) fusion(bf16[256,4096]{1,0:T(8,128)(2,1)S(1)} %copy-done.2, f32[256,896]{1,0:T(8,128)S(1)} %fusion.9, f32[256,896]{1,0:T(8,128)S(1)} %fusion.3, f32[256,896]{1,0:T(8,128)S(1)} %copy-done.3), kind=kOutput, calls=%fused_computation.5 | convolution fusion | flops 1888681984 | bytes 19529732 | tf_op jit(solution)/shard_map/dot_general | solution.py:15
  97.9 8.3 %multiply_reduce_fusion.1 = (f32[]{:T(128)}, f32[896,4096]{1,0:T(8,128)}) fusion(bf16[256,4096]{1,0:T(8,128)(2,1)S(1)} %copy-done.2, f32[256,896]{1,0:T(8,128)S(1)} %fusion.3, f32[256,896]{1,0:T(8,128)S(1)} %fusion.9), kind=kOutput, calls=%fused_computation.4 | convolution fusion | flops 1887764480 | bytes 18612228 | tf_op jit(solution)/shard_map/dot_general | solution.py:15
  107.5 9.8 %multiply_reduce_fusion = (f32[]{:T(128)}, f32[896,4096]{1,0:T(8,128)}) fusion(bf16[256,896]{1,0:T(8,128)(2,1)} %copy-done.5, bf16[256,4096]{1,0:T(8,128)(2,1)} %all-gather.5.cloned.1.call-done), kind=kOutput, calls=%fused_computation.3 | convolution fusion | flops 1886388224 | bytes 17235972 | tf_op jit(solution)/shard_map/dot_general | solution.py:15
  118.0 39.8 %psum.7 = f32[]{:T(128)} all-reduce(f32[]{:T(128)S(6)} %add.35), channel_id=1, replica_groups=mesh['dp'=2,'expert'=4,'ffn'=4] {'dp','expert','ffn'}, use_global_device_ids=true, to_apply=%region_8.9 | all-reduce | flops 1 | bytes 8 | tf_op jit(solution)/shard_map/psum | solution.py:82
  158.4 15.5 %fusion = (bf16[1,896,4096]{2,1,0:T(8,128)(2,1)}, bf16[1,896,4096]{2,1,0:T(8,128)(2,1)}) fusion(f32[896,4096]{1,0:T(8,128)} %get-tuple-element.7, f32[]{:T(128)S(6)} %rsqrt.3, f32[896,4096]{1,0:T(8,128)} %get-tuple-element.9), kind=kLoop, calls=%fused_computation.6 | loop fusion | flops 14680064 | bytes 44040196 | tf_op jit(solution)/shard_map/broadcast_in_dim | solution.py:99
  173.9 3.6 %all-to-all-start.1 = ((bf16[4,64,512]{2,1,0:T(8,128)(2,1)}), bf16[4,64,512]{2,1,0:T(8,128)(2,1)S(1)}, u32[]{:S(2)}, u32[]{:S(2)}) async-start(bf16[4,64,512]{2,1,0:T(8,128)(2,1)} %bitcast.53), calls=%async_computation.2 | async-start | bytes 524288 | tf_op jit(solution)/shard_map/all_to_all | solution.py:89
  177.5 10.3 %fusion.2 = bf16[1,896,4096]{2,1,0:T(8,128)(2,1)} fusion(f32[896,4096]{1,0:T(8,128)} %get-tuple-element.11, f32[]{:T(128)S(6)} %rsqrt.3), kind=kLoop, calls=%fused_computation.8 | loop fusion | flops 7340032 | bytes 22020100 | tf_op jit(solution)/shard_map/broadcast_in_dim | solution.py:101
  187.7 0.9 fusion.18
  (23 shorter events, 0.1 us)
Async XLA Ops:
  7.2 2.7 %copy-start = (bf16[128,4096]{1,0:T(8,128)(2,1)S(1)}, bf16[128,4096]{1,0:T(8,128)(2,1)}, u32[]{:S(2)}) copy-start(bf16[128,4096]{1,0:T(8,128)(2,1)} %param.7) | copy-start | bytes 3145732
  7.2 18.6 %copy-start.4 = (bf16[128,4096]{1,0:T(8,128)(2,1)S(1)}, bf16[128,4096]{1,0:T(8,128)(2,1)}, u32[]{:S(2)}) copy-start(bf16[128,4096]{1,0:T(8,128)(2,1)} %param.10) | copy-start | bytes 3145732
  7.2 18.8 %copy-start.6 = (f32[128,2]{0,1:T(2,128)S(1)}, f32[128,2]{0,1:T(2,128)}, u32[]{:S(2)}) copy-start(f32[128,2]{0,1:T(2,128)} %param.9) | copy-start | bytes 3076
  7.2 45.9 %all-gather.3.cloned.1.call-start = ((), (), s32[]{:S(2)}) async-start(), calls=%async_computation.4 | async-start | bytes 2359296 | tf_op jit(solution)/shard_map/all_gather | solution.py:61
  25.8 57.4 %all-gather.5.cloned.1.call-start = ((), (), s32[]{:S(2)}) async-start(), calls=%async_computation.6 | async-start | bytes 2359296 | tf_op jit(solution)/shard_map/all_gather | solution.py:64
  38.0 135.9 %reduce-scatter.2.cloned.1.call-start = ((), (), s32[]{:S(2)}) async-start(), calls=%async_computation.5 | async-start | bytes 2359296 | tf_op jit(solution)/shard_map/reduce_scatter | solution.py:85
  53.1 6.2 %copy-start.2 = (bf16[256,4096]{1,0:T(8,128)(2,1)S(1)}, bf16[256,4096]{1,0:T(8,128)(2,1)}, u32[]{:S(2)}) copy-start(bf16[256,4096]{1,0:T(8,128)(2,1)} %all-gather.3.cloned.1.call-done) | copy-start | bytes 6291460
  53.1 13.7 %slice-start = ((s8[7340032]{0:T(1024)(128)(4,1)}), s8[4194304]{0:T(1024)(128)(4,1)S(1)}, s32[]{:S(2)}) async-start(s8[7340032]{0:T(1024)(128)(4,1)} %bitcast.55), calls=%async_computation.7 | async-start | bytes 8388608
  59.4 7.5 %slice-start.1 = ((s8[7340032]{0:T(1024)(128)(4,1)}), s8[3145728]{0:T(1024)(128)(4,1)S(1)}, s32[]{:S(2)}) async-start(s8[7340032]{0:T(1024)(128)(4,1)} %bitcast.55), calls=%async_computation.8 | async-start | bytes 6291456
  66.1 0.8 copy-start.5
  83.1 6.2 %copy-start.3 = (f32[256,896]{1,0:T(8,128)S(1)}, f32[256,896]{1,0:T(8,128)}, u32[]{:S(2)}) copy-start(f32[256,896]{1,0:T(8,128)} %get-tuple-element.5) | copy-start | bytes 2752516
  173.9 13.8 %all-to-all-start.1 = ((bf16[4,64,512]{2,1,0:T(8,128)(2,1)}), bf16[4,64,512]{2,1,0:T(8,128)(2,1)S(1)}, u32[]{:S(2)}, u32[]{:S(2)}) async-start(bf16[4,64,512]{2,1,0:T(8,128)(2,1)} %bitcast.53), calls=%async_computation.2 | async-start | bytes 524288 | tf_op jit(solution)/shard_map/all_to_all | solution.py:89
  177.5 11.2 %copy-start.1 = (bf16[128,4096]{1,0:T(8,128)(2,1)S(1)}, bf16[128,4096]{1,0:T(8,128)(2,1)}, u32[]{:S(2)}) copy-start(bf16[128,4096]{1,0:T(8,128)(2,1)} %param.7) | copy-start | bytes 3145732
Sparse Core Ops, SparseCore 0:
  25.9 27.1 all-gather.2
  55.0 28.0 all-gather.4
  87.0 41.6 reduce-scatter.1
where the time goes:
time: 196 us; the launch traced here: 195 us
  blocking collectives  66 us (34%)
  matrix products  51.9 us (26%)
  other arithmetic  28.4 us (14%)
  waiting for transfers between devices  27.5 us (14%)
  between operations  16.5 us (8%)
  starting transfers between devices  3.85 us (2%)
    psum x1, blocking collectives, on_device(): lax.psum(squares_of(grad_gate) + squares_of(grad_up) + squares_of(grad_do...  39.8 us
    dot_general x5, matrix products, against_rows(): lax.dot_general(left_rows, right_rows, (((0,), (0,)), ((), ())), preferre...  28.3 us
    dot_general x3, matrix products, across_width(): lax.dot_general(left_rows, weight, (((1,), (1,)), ((), ())), preferred_el...  19.1 us
    broadcast_in_dim x1, other arithmetic, on_device(): (grad_gate * inv_rms).astype(jnp.bfloat16)[None]  15.5 us
    all_to_all x1, blocking collectives, on_device(): lax.all_to_all(token_part, 'expert', split_axis=0, concat_axis=0, tiled=T...  15.1 us
    all_gather x1, waiting for transfers between devices, on_device(): lax.all_gather(received[0].reshape(slot_count, column_width), ('dp', 'ffn...  14.9 us
    all_gather x1, waiting for transfers between devices, on_device(): lax.all_gather(received[1].reshape(slot_count, column_width), ('dp', 'ffn...  12.6 us
    all_to_all x1, blocking collectives, on_device(): lax.all_to_all(grad_part, 'expert', split_axis=0, concat_axis=0, tiled=True)  11.1 us
  transfers between devices with their start and end apart: 4, of which 2 were waited for; matrix products, arithmetic and copies ran while one was open for 39% of the time, Pallas kernels for 0%

commit v1 on v0

v1 whole, which is shorter than its diff:
```python
import functools

import jax
import jax.numpy as jnp
from jax import lax
from jax.experimental import pallas as pl
from jax.experimental.pallas import tpu as pltpu
from jax.sharding import PartitionSpec as P

CORES = 2


def silu_parts(pre_act):
    sigmoid_value = jax.nn.sigmoid(pre_act)
    return (pre_act * sigmoid_value, sigmoid_value * (1.0 + pre_act * (1.0 - sigmoid_value)))


def against_rows(left_rows, right_rows):
    return lax.dot_general(
        left_rows, right_rows, (((0,), (0,)), ((), ())), preferred_element_type=jnp.float32
    )


def across_width(left_rows, weight):
    return lax.dot_general(
        left_rows, weight, (((1,), (1,)), ((), ())), preferred_element_type=jnp.float32
    )


def remote(src, dst, send_sem, recv_sem, device):
    return pltpu.make_async_remote_copy(
        src_ref=src,
        dst_ref=dst,
        send_sem=send_sem,
        recv_sem=recv_sem,
        device_id=device,
        device_id_type=pl.DeviceIdType.MESH,
    )


class Place:
    def __init__(self, ny, nz, nx, width):
        self.ny, self.nz, self.nx, self.width = ny, nz, nx, width
        self.y = lax.axis_index("dp")
        self.z = lax.axis_index("expert")
        ffn = lax.axis_index("ffn")
        self.x, self.c = ffn // CORES, lax.rem(ffn, CORES)

    def at(self, dy=0, dz=0, dx=0, other=False):
        core = 1 - self.c if other else self.c
        return (
            lax.rem(self.y + dy + self.ny, self.ny),
            lax.rem(self.z + dz + self.nz, self.nz),
            lax.rem(self.x + dx + self.nx, self.nx) * CORES + core,
        )

    def cols(self, dy=0, dx=0, other=False):
        y, _, ffn = self.at(dy, 0, dx, other)
        group = y * (self.nx * CORES) + ffn
        return pl.ds(pl.multiple_of(group * self.width, self.width), self.width)

    def greet(self):
        peers = [self.at(other=True)]
        peers += [self.at(dx=i) for i in range(1, self.nx)]
        peers += [self.at(dy=k) for k in range(1, self.ny)]
        peers += [self.at(dz=j) for j in range(1, self.nz)]
        return peers

    def enter(self, more=()):
        barrier = pltpu.get_barrier_semaphore()
        peers = self.greet() + list(more)
        for peer in peers:
            pl.semaphore_signal(
                barrier, inc=1, device_id=peer, device_id_type=pl.DeviceIdType.MESH
            )
        pl.semaphore_wait(barrier, len(peers))


def dispatch_kernel(
    ny, nz, nx, cap, width, tok, grad, rows, grads,
    own_sem, zs, zr, xs, xr, ys, yr, us, ur, ls, lr, ds, dr,
):
    here = Place(ny, nz, nx, width)
    here.enter()
    source, target = (tok, grad), (rows, grads)
    pending = []

    def block(dz):
        return pl.multiple_of(here.at(dz=dz)[1] * cap, cap)

    for a in range(2):
        for j in range(1, nz):
            unit = a * (nz - 1) + j - 1
            copy = remote(
                source[a].at[pl.ds(block(j), cap), here.cols()],
                target[a].at[pl.ds(block(0), cap), here.cols()],
                zs.at[unit], zr.at[unit], here.at(dz=j),
            )
            copy.start()
            pending.append(copy)
    local = []
    for a in range(2):
        copy = pltpu.make_async_copy(
            source[a].at[pl.ds(block(0), cap), :],
            target[a].at[pl.ds(block(0), cap), :],
            own_sem.at[a],
        )
        copy.start()
        local.append(copy)

    def piece(unit, dy=0, dx=0, other=False, half=None):
        a, j = unit // (nz - 1), unit % (nz - 1) + 1
        first, count = block(-j), cap
        if half is not None:
            count = cap // 2
            first = pl.multiple_of(first + half * count, count)
        return target[a].at[pl.ds(first, count), here.cols(dy, dx, other)]

    def push(ref, send_sem, recv_sem, device):
        copy = remote(ref, ref, send_sem, recv_sem, device)
        copy.start()
        pending.append(copy)

    def arrived(ref, send_sem, recv_sem):
        remote(ref, ref, send_sem, recv_sem, here.at(other=True)).wait_recv()

    def first(u):
        arrived(piece(u), zs.at[u], zr.at[u])
        for i in range(1, nx):
            push(piece(u), xs.at[u, i - 1], xr.at[u, i - 1], here.at(dx=i))
        for k in range(1, ny):
            push(piece(u), ys.at[u, k - 1], yr.at[u, k - 1], here.at(dy=k))
        push(piece(u), ds.at[u, 0], dr.at[u, 0], here.at(other=True))

    def second(u):
        for i in range(1, nx):
            arrived(piece(u, dx=-i), xs.at[u, i - 1], xr.at[u, i - 1])
            for k in range(1, ny):
                at = (i - 1) * (ny - 1) + k - 1
                push(piece(u, dx=-i, half=0), us.at[u, at], ur.at[u, at], here.at(dy=k))
            push(piece(u, dx=-i), ds.at[u, i], dr.at[u, i], here.at(other=True))
        for k in range(1, ny):
            arrived(piece(u, dy=-k), ys.at[u, k - 1], yr.at[u, k - 1])
            for i in range(1, nx):
                at = (i - 1) * (ny - 1) + k - 1
                push(piece(u, dy=-k, half=1), ls.at[u, at], lr.at[u, at], here.at(dx=i))
            push(piece(u, dy=-k), ds.at[u, k * nx], dr.at[u, k * nx], here.at(other=True))

    def third(u):
        for i in range(1, nx):
            for k in range(1, ny):
                at = (i - 1) * (ny - 1) + k - 1
                arrived(piece(u, -k, -i, half=0), us.at[u, at], ur.at[u, at])
                arrived(piece(u, -k, -i, half=1), ls.at[u, at], lr.at[u, at])
                to = k * nx + i
                push(piece(u, -k, -i), ds.at[u, to], dr.at[u, to], here.at(other=True))

    def fourth(u):
        for i in range(nx):
            for k in range(ny):
                to = k * nx + i
                arrived(piece(u, -k, -i, True), ds.at[u, to], dr.at[u, to])

    units = 2 * (nz - 1)
    stages = (first, second, third, fourth)
    for step in range(units + len(stages) - 1):
        for late, stage in enumerate(stages):
            if 0 <= step - late < units:
                stage(step - late)
    for copy in local:
        copy.wait()
    for copy in pending:
        copy.wait_send()


def dispatch(sizes, tok, grad):
    ny, nz, nx, cap, width = sizes
    units, chips = 2 * (nz - 1), nx * ny
    diag = max(1, (nx - 1) * (ny - 1))
    dma = pltpu.SemaphoreType.DMA
    pair = lambda *shape: [dma(shape), dma(shape)]
    vmem = pl.BlockSpec(memory_space=pltpu.VMEM)
    return pl.pallas_call(
        functools.partial(dispatch_kernel, *sizes),
        out_shape=[jax.ShapeDtypeStruct(tok.shape, tok.dtype)] * 2,
        in_specs=[vmem] * 2,
        out_specs=[vmem] * 2,
        scratch_shapes=[
            dma((2,)),
            *pair(units), *pair(units, max(1, nx - 1)), *pair(units, max(1, ny - 1)),
            *pair(units, diag), *pair(units, diag), *pair(units, chips),
        ],
        compiler_params=pltpu.CompilerParams(collective_id=0, has_side_effects=True),
    )(tok, grad)


def combine_kernel(
    ny, nz, nx, cap, width, part, sq, ret, sq_out,
    pair, out_buf, in_buf, acc, summed, sq_own, sq_in,
    ps, pr, cs, cr, zs, zr, ss, sr,
):
    here = Place(ny, nz, nx, width)
    for_diag = [(k, i) for k in range(1, ny) for i in range(1, nx)]
    here.enter([here.at(k, 0, i) for k, i in for_diag])
    order = for_diag + [(0, i) for i in range(1, nx)] + [(k, 0) for k in range(1, ny)] + [(0, 0)]
    pending = []

    def started(copy):
        copy.start()
        pending.append(copy)
        return copy

    partner = here.at(other=True)
    swaps = {}
    for k, i in order:
        o = k * nx + i
        swaps[o] = started(
            remote(part.at[:, here.cols(k, i, True)], pair.at[o], ps.at[o], pr.at[o], partner)
        )

    def stage(level, peers, base):
        for n, (to, _) in enumerate(peers):
            started(
                remote(sq_own.at[level], sq_in.at[base + n], ss.at[base + n], sr.at[base + n], to)
            )
        total = sq_own[level]
        for n in range(len(peers)):
            remote(
                sq_own.at[level], sq_in.at[base + n], ss.at[base + n], sr.at[base + n], partner
            ).wait_recv()
            total = total + sq_in[base + n]
        sq_own[level + 1] = total
        return base + len(peers)

    sq_own[0] = sq[...]
    base = stage(0, [(partner, 0)], 0)
    for k, i in order:
        o = k * nx + i
        swaps[o].wait_recv()
        total = part[:, here.cols(k, i)].astype(jnp.float32) + pair[o].astype(jnp.float32)
        if o == 0:
            acc[...] = total
        else:
            out_buf[o] = total.astype(jnp.bfloat16)
            started(
                remote(out_buf.at[o], in_buf.at[o], cs.at[o], cr.at[o], here.at(k, 0, i))
            )
    base = stage(1, [(here.at(dz=j), 0) for j in range(1, nz)], base)
    base = stage(2, [(here.at(dx=i), 0) for i in range(1, nx)], base)
    base = stage(3, [(here.at(dy=k), 0) for k in range(1, ny)], base)
    sq_out[...] = sq_own[4]
    for o in range(1, nx * ny):
        remote(out_buf.at[o], in_buf.at[o], cs.at[o], cr.at[o], partner).wait_recv()
    total = acc[...]
    for o in range(1, nx * ny):
        total = total + in_buf[o].astype(jnp.float32)
    summed[...] = total.astype(jnp.bfloat16)

    def block(dz):
        return pl.ds(pl.multiple_of(here.at(dz=dz)[1] * cap, cap), cap)

    backs = []
    for j in range(1, nz):
        backs.append(
            started(
                remote(
                    summed.at[block(j), :], ret.at[block(0), :],
                    zs.at[j - 1], zr.at[j - 1], here.at(dz=j),
                )
            )
        )
    ret[block(0), :] = summed[block(0), :]
    for copy in backs:
        copy.wait_recv()
    for copy in pending:
        copy.wait_send()


def combine(sizes, part, square):
    ny, nz, nx, cap, width = sizes
    slots, chips = nz * cap, nx * ny
    peers = 1 + (nz - 1) + (nx - 1) + (ny - 1)
    dma = pltpu.SemaphoreType.DMA
    twice = lambda count: [dma((count,)), dma((count,))]
    vmem = pl.BlockSpec(memory_space=pltpu.VMEM)
    flat = jnp.full((8, 128), square, jnp.float32)
    return pl.pallas_call(
        functools.partial(combine_kernel, *sizes),
        out_shape=[
            jax.ShapeDtypeStruct((slots, width), jnp.bfloat16),
            jax.ShapeDtypeStruct((8, 128), jnp.float32),
        ],
        in_specs=[vmem] * 2,
        out_specs=[vmem] * 2,
        scratch_shapes=[
            *[pltpu.VMEM((chips, slots, width), jnp.bfloat16)] * 3,
            pltpu.VMEM((slots, width), jnp.float32),
            pltpu.VMEM((slots, width), jnp.bfloat16),
            pltpu.VMEM((5, 8, 128), jnp.float32),
            pltpu.VMEM((peers, 8, 128), jnp.float32),
            *twice(chips), *twice(chips), *twice(max(1, nz - 1)), *twice(peers),
        ],
        compiler_params=pltpu.CompilerParams(
            collective_id=1, has_side_effects=True, vmem_limit_bytes=48 * 1024 * 1024
        ),
    )(part, flat)


def on_device(sizes, count, tokens, expert_ids, route_weight, cotangent, w_gate, w_up, w_down):
    ny, experts, nx, capacity, column_width = sizes
    tok_rows, feature_width = tokens.shape
    slot_count = experts * capacity
    chosen = expert_ids[:, :, None] == jnp.arange(experts, dtype=jnp.int32)[None, None, :]
    per_token = jnp.sum(chosen.astype(jnp.bfloat16), axis=1)
    row = jnp.arange(tok_rows, dtype=jnp.int32)
    before = (row[None, :] < row[:, None]).astype(jnp.bfloat16)
    earlier = jnp.dot(before, per_token, preferred_element_type=jnp.float32).astype(jnp.int32)
    position = jnp.sum(jnp.where(chosen, earlier[:, None, :], 0), axis=2)
    slot_index = expert_ids * capacity + position
    slots = jnp.arange(slot_count, dtype=jnp.int32)
    hot = [slot_index[:, k][None, :] == slots[:, None] for k in range(2)]
    hot_any = (hot[0] | hot[1]).astype(jnp.bfloat16)
    token_slots = jnp.dot(hot_any, tokens, preferred_element_type=jnp.float32).astype(jnp.bfloat16)
    picked_cot = jnp.dot(hot_any, cotangent, preferred_element_type=jnp.float32)
    slot_weight = jnp.sum(
        jnp.where(hot[0], route_weight[:, 0][None, :], 0.0)
        + jnp.where(hot[1], route_weight[:, 1][None, :], 0.0),
        axis=1,
    )
    grad_slots = (slot_weight[:, None] * picked_cot).astype(jnp.bfloat16)
    slot_rows, slot_grads = dispatch(sizes, token_slots, grad_slots)
    gate_weight, up_weight, down_weight = w_gate[0], w_up[0], w_down[0]
    pre_gate = across_width(slot_rows, gate_weight)
    pre_up = across_width(slot_rows, up_weight)
    activated, derivative = silu_parts(pre_gate)
    hidden = (activated * pre_up).astype(jnp.bfloat16)
    partial_value = jnp.dot(hidden, down_weight, preferred_element_type=jnp.float32)
    grad_hidden = across_width(slot_grads, down_weight)
    delta_gate = (grad_hidden * pre_up * derivative).astype(jnp.bfloat16)
    delta_up = (grad_hidden * activated).astype(jnp.bfloat16)
    gram_rows = across_width(slot_rows, slot_rows)
    gram_grads = across_width(slot_grads, slot_grads)
    gram_delta = across_width(delta_gate, delta_gate) + across_width(delta_up, delta_up)
    square = jnp.sum(gram_rows * gram_delta) + jnp.sum(gram_grads * across_width(hidden, hidden))
    returned_rows, square_all = combine(sizes, partial_value.astype(jnp.bfloat16), square)
    weight_hot = [h.astype(jnp.bfloat16) for h in hot]
    picked = [against_rows(h, returned_rows) for h in weight_hot]
    layer_out = (route_weight[:, 0:1] * picked[0] + route_weight[:, 1:2] * picked[1]).astype(
        jnp.bfloat16
    )
    inv_rms = lax.rsqrt(jnp.maximum(square_all[0, 0], 0.0) / count + 1e-06)
    return (
        layer_out,
        (against_rows(delta_gate, slot_rows) * inv_rms).astype(jnp.bfloat16)[None],
        (against_rows(delta_up, slot_rows) * inv_rms).astype(jnp.bfloat16)[None],
        (against_rows(hidden, slot_grads) * inv_rms).astype(jnp.bfloat16)[None],
    )


def solution(mesh):
    ny, nz, nx = mesh.shape["dp"], mesh.shape["expert"], mesh.shape["ffn"] // CORES

    def body(*args):
        tok_rows, feature_width = args[0].shape
        sizes = (ny, nz, nx, tok_rows // 2, feature_width // (ny * nx * CORES))
        count = 3.0 * nz * args[4].shape[1] * (ny * nx * CORES) * feature_width
        return on_device(sizes, count, *args)

    return jax.shard_map(
        body,
        mesh=mesh,
        in_specs=(
            P("expert", None),
            P("expert", None),
            P("expert", None),
            P("expert", None),
            P("expert", ("dp", "ffn"), None),
            P("expert", ("dp", "ffn"), None),
            P("expert", ("dp", "ffn"), None),
        ),
        out_specs=(
            P("expert", ("dp", "ffn")),
            P("expert", ("dp", "ffn"), None),
            P("expert", ("dp", "ffn"), None),
            P("expert", ("dp", "ffn"), None),
        ),
        check_vma=False,
    )
```

time: 196 us -> 114 us (0.58)
  blocking collectives: 66 us -> 0 us
  Pallas kernels: 0 us -> 63.8 us
  waiting for transfers between devices: 27.5 us -> 0 us
  other arithmetic: 28.4 us -> 2.35 us
  between operations: 16.5 us -> 2.87 us
  matrix products: 51.9 us -> 43.4 us
  starting transfers between devices: 3.85 us -> 0 us
    pallas_call x0 -> x2, Pallas kernels: none -> 63.8 us  [the longest x1 34.5 us: dispatch(): pl.pallas_call(functools.partial(dispatch_kernel, *sizes), out_shape=[jax...]
    psum x1 -> x0, blocking collectives: 39.8 us -> none  [on_device(): lax.psum(squares_of(grad_gate) + squares_of(grad_up) + squares_of(grad_do...]
    all_gather x2 -> x0, waiting for transfers between devices: 27.5 us -> none  [the longest x1 14.9 us: on_device(): lax.all_gather(received[0].reshape(slot_count, column_width), ('dp', 'ffn...]
    all_to_all x2 -> x0, blocking collectives: 26.2 us -> none  [the longest x1 15.1 us: on_device(): lax.all_to_all(token_part, 'expert', split_axis=0, concat_axis=0, tiled=T...]
    broadcast_in_dim x2 -> x0, other arithmetic: 25.8 us -> none  [the longest x1 15.5 us: on_device(): (grad_gate * inv_rms).astype(jnp.bfloat16)[None]]
    dot_general x5, matrix products: 28.3 us -> 16.8 us  [against_rows(): lax.dot_general(left_rows, right_rows, (((0,), (0,)), ((), ())), preferre...]
    all_to_all x1 -> x0, starting transfers between devices: 3.55 us -> none  [on_device(): lax.all_to_all(summed, 'expert', split_axis=0, concat_axis=0, tiled=True)]
    dot_general x1 -> x3, matrix products: 0.93 us -> 4.17 us  [the longest x1 2.03 us: on_device(): picked_cot = jnp.dot(hot_any, cotangent, preferred_element_type=jnp.float32)]
  transfers between devices with their start and end apart: 4 -> 0, of which waited for: 2 -> 0; matrix products, arithmetic and copies ran while one was open for 39% -> 0% of each run, Pallas kernels for 0% -> 0%
where the time goes in v1:
time: 114 us
  Pallas kernels  63.8 us (56%)
  matrix products  43.4 us (38%)
  between operations  2.87 us (3%)
  other arithmetic  2.35 us (2%)
  local copies, waits for them, and re-layouts  1.48 us (1%)
    pallas_call x1, Pallas kernels, dispatch(): pl.pallas_call(functools.partial(dispatch_kernel, *sizes), out_shape=[jax...  34.5 us
    pallas_call x1, Pallas kernels, combine(): pl.pallas_call(functools.partial(combine_kernel, *sizes), out_shape=[jax....  29.3 us
    dot_general x8, matrix products, across_width(): lax.dot_general(left_rows, weight, (((1,), (1,)), ((), ())), preferred_el...  16.9 us
    dot_general x5, matrix products, against_rows(): lax.dot_general(left_rows, right_rows, (((0,), (0,)), ((), ())), preferre...  16.8 us
    dot_general x1, matrix products, on_device(): jnp.dot(hidden, down_weight, preferred_element_type=jnp.float32)  5.59 us

profile of v1, /device:TPU:0, one launch (start us, length us, event | category | flops | bytes accessed | tf_op | source)
XLA Modules:
  0.0 113.9 jit_solution(13262625010690936656)
XLA Ops:
  0.6 0.0 copy-start
  0.7 0.8 fusion.31
  1.5 0.1 convolution_convert_fusion.1
  1.6 0.7 select_reduce_fusion
  2.3 0.7 multiply_add_fusion
  3.0 0.8 slice_bitcast_fusion.3
  3.8 0.1 add_reduce_fusion
  3.9 2.0 %fusion.14.grad = bf16[256,4096]{1,0:T(8,128)(2,1)} fusion(bf16[128,4096]{1,0:T(8,128)(2,1)S(1)} %copy-done, f32[256]{0:T(256)S(1)} %add_reduce_fusion, s32[128]{0:T(128)S(1)} %get-tuple-element.18, s32[128]{0:T(128)S(1)} %get-tuple-element.17), kind=kOutput, calls=%fused_computation.17 | convolution fusion | flops 270630912 | bytes 3147776 | tf_op jit(solution)/shard_map/dot_general | solution.py:324
  5.9 2.0 %convolution_convert_fusion.tok = bf16[256,4096]{1,0:T(8,128)(2,1)} fusion(bf16[128,4096]{1,0:T(8,128)(2,1)S(1)} %copy-done.10, s32[128]{0:T(128)S(1)} %get-tuple-element.18, s32[128]{0:T(128)S(1)} %get-tuple-element.17), kind=kOutput, calls=%fused_computation.16 | convolution fusion | flops 269582336 | bytes 3146752 | tf_op jit(solution)/shard_map/dot_general | solution.py:323
  8.0 34.5 %shard_map.102 = (bf16[256,4096]{1,0:T(8,128)(2,1)}, bf16[256,4096]{1,0:T(8,128)(2,1)}) custom-call(bf16[256,4096]{1,0:T(8,128)(2,1)} %convolution_convert_fusion.tok, bf16[256,4096]{1,0:T(8,128)(2,1)} %fusion.14.grad), custom_call_target="tpu_custom_call" | custom-call | tf_op jit(solution)/shard_map/pallas_call | solution.py:183
  42.4 3.1 %fusion.34 = f32[256,256]{1,0:T(8,128)S(1)} fusion(bf16[256,4096]{1,0:T(8,128)(2,1)} %get-tuple-element.9), kind=kOutput, calls=%fused_computation.55 | convolution fusion | flops 536870912 | bytes 2359296 | tf_op jit(solution)/shard_map/dot_general | solution.py:25
  45.6 0.0 slice-start
  45.6 0.7 fusion.32
  46.3 0.0 slice-start.1
  46.3 0.0 slice-start.2
  46.4 5.8 %fusion.4 = f32[256,896]{1,0:T(8,128)S(1)} fusion(bf16[256,4096]{1,0:T(8,128)(2,1)S(1)} %copy-done.1, bf16[1,896,4096]{2,1,0:T(8,128)(2,1)} %param.12), kind=kOutput, calls=%fused_computation.7 | convolution fusion | flops 1879048192 | bytes 10354688 | tf_op jit(solution)/shard_map/dot_general | solution.py:25
  52.2 0.0 slice-start.3
  52.2 2.4 %fusion.6 = f32[256,896]{1,0:T(8,128)S(1)} fusion(bf16[256,4096]{1,0:T(8,128)(2,1)S(1)} %copy-done.1, bf16[1,896,4096]{2,1,0:T(8,128)(2,1)S(1)} %bitcast.56), kind=kOutput, calls=%fused_computation.9 | convolution fusion | flops 1879048192 | bytes 10354688 | tf_op jit(solution)/shard_map/dot_general | solution.py:25
  54.6 0.1 slice-done.3
  54.7 2.6 %multiply_convert_fusion.3 = (bf16[256,896]{1,0:T(8,128)(2,1)S(1)}, bf16[256,896]{1,0:T(8,128)(2,1)S(1)}, bf16[256,896]{1,0:T(8,128)(2,1)S(1)}) fusion(f32[256,896]{1,0:T(8,128)S(1)} %fusion.6, f32[256,896]{1,0:T(8,128)S(1)} %fusion.4, bf16[256,4096]{1,0:T(8,128)(2,1)S(1)} %copy-done.2, bf16[1,896,4096]{2,1,0:T(8,128)(2,1)S(1)} %bitcast.58), kind=kOutput, calls=%fused_computation.26 | convolution fusion | flops 1882488832 | bytes 12648448 | tf_op jit(solution)/shard_map/dot_general | solution.py:25
  57.3 0.0 copy-start.6
  57.4 1.0 fusion.19
  58.4 0.3 fusion.33
  58.7 0.9 fusion.20
  60.9 5.6 %fusion.11.part = bf16[256,4096]{1,0:T(8,128)(2,1)S(1)} fusion(bf16[256,896]{1,0:T(8,128)(2,1)} %copy-done.8, bf16[1,896,4096]{2,1,0:T(8,128)(2,1)} %param.13), kind=kOutput, calls=%fused_computation.15 | convolution fusion | flops 1880096768 | bytes 9895936 | tf_op jit(solution)/shard_map/dot_general | solution.py:337
  66.6 29.3 %shard_map.103 = (bf16[256,512]{1,0:T(8,128)(2,1)S(1)}, f32[8,128]{1,0:T(8,128)S(1)}) custom-call(bf16[256,4096]{1,0:T(8,128)(2,1)S(1)} %fusion.11.part, f32[8,128]{1,0:T(8,128)S(1)} %broadcast_in_dim.58.sq), custom_call_target="tpu_custom_call" | custom-call | tf_op jit(solution)/shard_map/pallas_call | solution.py:287
  95.9 0.5 slice.21
  97.1 0.2 convolution_multiply_fusion.2
  97.3 0.9 fusion.17
  98.2 5.3 %fusion.10 = bf16[1,896,4096]{2,1,0:T(8,128)(2,1)} fusion(f32[]{:T(128)} %bitcast.7, bf16[256,896]{1,0:T(8,128)(2,1)S(1)} %copy-done.9, bf16[256,4096]{1,0:T(8,128)(2,1)S(1)} %copy-done.3), kind=kOutput, calls=%fused_computation.13 | convolution fusion | flops 1886388224 | bytes 9895940 | tf_op jit(solution)/shard_map/dot_general | solution.py:19
  103.6 5.2 %fusion.9 = bf16[1,896,4096]{2,1,0:T(8,128)(2,1)} fusion(f32[]{:T(128)} %bitcast.7, bf16[256,896]{1,0:T(8,128)(2,1)S(1)} %copy-done.7, bf16[256,4096]{1,0:T(8,128)(2,1)S(1)} %copy-done.1), kind=kOutput, calls=%fused_computation.12 | convolution fusion | flops 1886388224 | bytes 9895940 | tf_op jit(solution)/shard_map/dot_general | solution.py:19
  108.8 5.2 %fusion.8 = bf16[1,896,4096]{2,1,0:T(8,128)(2,1)} fusion(f32[]{:T(128)} %bitcast.7, bf16[256,896]{1,0:T(8,128)(2,1)S(1)} %copy-done.5, bf16[256,4096]{1,0:T(8,128)(2,1)S(1)} %copy-done.1), kind=kOutput, calls=%fused_computation.11 | convolution fusion | flops 1886388224 | bytes 9895940 | tf_op jit(solution)/shard_map/dot_general | solution.py:19
  (27 shorter events, 0.1 us)
Async XLA Ops:
  0.6 3.3 %copy-start = (bf16[128,4096]{1,0:T(8,128)(2,1)S(1)}, bf16[128,4096]{1,0:T(8,128)(2,1)}, u32[]{:S(2)}) copy-start(bf16[128,4096]{1,0:T(8,128)(2,1)} %param.10) | copy-start | bytes 3145732
  0.6 5.3 %copy-start.10 = (bf16[128,4096]{1,0:T(8,128)(2,1)S(1)}, bf16[128,4096]{1,0:T(8,128)(2,1)}, u32[]{:S(2)}) copy-start(bf16[128,4096]{1,0:T(8,128)(2,1)} %param.7) | copy-start | bytes 3145732
  42.4 3.1 %copy-start.1 = (bf16[256,4096]{1,0:T(8,128)(2,1)S(1)}, bf16[256,4096]{1,0:T(8,128)(2,1)}, u32[]{:S(2)}) copy-start(bf16[256,4096]{1,0:T(8,128)(2,1)} %get-tuple-element.8) | copy-start | bytes 6291460
  45.6 6.6 %slice-start = ((s8[7340032]{0:T(1024)(128)(4,1)}), s8[4194304]{0:T(1024)(128)(4,1)S(1)}, s32[]{:S(2)}) async-start(s8[7340032]{0:T(1024)(128)(4,1)} %bitcast.55), calls=%async_computation | async-start | bytes 8388608
  46.3 5.9 %slice-start.1 = ((s8[7340032]{0:T(1024)(128)(4,1)}), s8[3145728]{0:T(1024)(128)(4,1)S(1)}, s32[]{:S(2)}) async-start(s8[7340032]{0:T(1024)(128)(4,1)} %bitcast.55), calls=%async_computation.1 | async-start | bytes 6291456
  46.3 8.3 %slice-start.2 = ((s8[7340032]{0:T(1024)(128)(4,1)}), s8[4194304]{0:T(1024)(128)(4,1)S(1)}, s32[]{:S(2)}) async-start(s8[7340032]{0:T(1024)(128)(4,1)} %bitcast.57), calls=%async_computation.2 | async-start | bytes 8388608
  52.2 2.4 %copy-start.2 = (bf16[256,4096]{1,0:T(8,128)(2,1)S(1)}, bf16[256,4096]{1,0:T(8,128)(2,1)}, u32[]{:S(2)}) copy-start(bf16[256,4096]{1,0:T(8,128)(2,1)} %get-tuple-element.9) | copy-start | bytes 6291460
  52.2 2.5 %slice-start.3 = ((s8[7340032]{0:T(1024)(128)(4,1)}), s8[3145728]{0:T(1024)(128)(4,1)S(1)}, s32[]{:S(2)}) async-start(s8[7340032]{0:T(1024)(128)(4,1)} %bitcast.57), calls=%async_computation.3 | async-start | bytes 6291456
  57.3 1.0 copy-start.4
  57.3 1.4 %copy-start.6 = (bf16[256,896]{1,0:T(8,128)(2,1)}, bf16[256,896]{1,0:T(8,128)(2,1)S(1)}, u32[]{:S(2)}) copy-start(bf16[256,896]{1,0:T(8,128)(2,1)S(1)} %get-tuple-element.12) | copy-start | bytes 1376260
  57.3 1.4 %copy-start.8 = (bf16[256,896]{1,0:T(8,128)(2,1)}, bf16[256,896]{1,0:T(8,128)(2,1)S(1)}, u32[]{:S(2)}) copy-start(bf16[256,896]{1,0:T(8,128)(2,1)S(1)} %get-tuple-element.14) | copy-start | bytes 1376260
  66.5 31.7 %copy-start.3 = (bf16[256,4096]{1,0:T(8,128)(2,1)S(1)}, bf16[256,4096]{1,0:T(8,128)(2,1)}, u32[]{:S(2)}) copy-start(bf16[256,4096]{1,0:T(8,128)(2,1)} %get-tuple-element.9) | copy-start | bytes 6291460
  66.5 31.7 %copy-start.9 = (bf16[256,896]{1,0:T(8,128)(2,1)S(1)}, bf16[256,896]{1,0:T(8,128)(2,1)}, u32[]{:S(2)}) copy-start(bf16[256,896]{1,0:T(8,128)(2,1)} %copy-done.8) | copy-start | bytes 1376260
  98.2 5.4 %copy-start.7 = (bf16[256,896]{1,0:T(8,128)(2,1)S(1)}, bf16[256,896]{1,0:T(8,128)(2,1)}, u32[]{:S(2)}) copy-start(bf16[256,896]{1,0:T(8,128)(2,1)} %copy-done.6) | copy-start | bytes 1376260
  103.6 5.2 %copy-start.5 = (bf16[256,896]{1,0:T(8,128)(2,1)S(1)}, bf16[256,896]{1,0:T(8,128)(2,1)}, u32[]{:S(2)}) copy-start(bf16[256,896]{1,0:T(8,128)(2,1)} %copy-done.4) | copy-start | bytes 1376260

commit v2 on v1

--- a/solution.py
+++ b/solution.py
@@ -25,6 +25,10 @@
     return lax.dot_general(
         left_rows, weight, (((1,), (1,)), ((), ())), preferred_element_type=jnp.float32
     )
+
+
+def along(left, right):
+    return jnp.dot(left, right, preferred_element_type=jnp.float32)
 
 
 def remote(src, dst, send_sem, recv_sem, device):
@@ -76,11 +80,26 @@
         pl.semaphore_wait(barrier, len(peers))
 
 
+def against_slots(weight, slots, out):
+    tile = weight.shape[0] // 2
+
+    def half(n, carry):
+        at = pl.ds(pl.multiple_of(n * tile, tile), tile)
+        out[at, :] = across_width(weight[at, :], slots[...])
+        return carry
+
+    lax.fori_loop(0, 2, half, 0)
+
+
 def dispatch_kernel(
-    ny, nz, nx, cap, width, tok, grad, rows, grads,
-    own_sem, zs, zr, xs, xr, ys, yr, us, ur, ls, lr, ds, dr,
+    ny, nz, nx, cap, width, tok, grad, wg, wu, wd, rows, grads, gate_t, up_t, hid_t, part,
+    wg_v, wu_v, wd_v, w_sem, own_sem, zs, zr, xs, xr, ys, yr, us, ur, ls, lr, ds, dr,
 ):
     here = Place(ny, nz, nx, width)
+    loads = []
+    for n, (weight, held) in enumerate(((wg, wg_v), (wu, wu_v), (wd, wd_v))):
+        loads.append(pltpu.make_async_copy(weight, held, w_sem.at[n]))
+        loads[-1].start()
     here.enter()
     source, target = (tok, grad), (rows, grads)
     pending = []
@@ -161,19 +180,45 @@
                 to = k * nx + i
                 arrived(piece(u, -k, -i, True), ds.at[u, to], dr.at[u, to])
 
+    def gate():
+        local[0].wait()
+        loads[0].wait()
+        against_slots(wg_v, rows, gate_t)
+
+    def up():
+        loads[1].wait()
+        against_slots(wu_v, rows, up_t)
+        activated, _ = silu_parts(gate_t[...])
+        hid_t[...] = (activated * up_t[...]).astype(jnp.bfloat16)
+
+    def down():
+        loads[2].wait()
+        tile = rows.shape[1] // 8
+
+        def columns(n, carry):
+            at = pl.ds(pl.multiple_of(n * tile, tile), tile)
+            part[:, at] = against_rows(hid_t[...], wd_v[:, at]).astype(jnp.bfloat16)
+            return carry
+
+        lax.fori_loop(0, 8, columns, 0)
+
+    work = [gate, up, down]
     units = 2 * (nz - 1)
     stages = (first, second, third, fourth)
     for step in range(units + len(stages) - 1):
         for late, stage in enumerate(stages):
             if 0 <= step - late < units:
                 stage(step - late)
-    for copy in local:
-        copy.wait()
+        if step >= nz + 1 and work:
+            work.pop(0)()
+    for task in work:
+        task()
+    local[1].wait()
     for copy in pending:
         copy.wait_send()
 
 
-def dispatch(sizes, tok, grad):
+def dispatch(sizes, tok, grad, wg, wu, wd):
     ny, nz, nx, cap, width = sizes
     units, chips = 2 * (nz - 1), nx * ny
     diag = max(1, (nx - 1) * (ny - 1))
@@ -182,25 +227,36 @@
     vmem = pl.BlockSpec(memory_space=pltpu.VMEM)
     return pl.pallas_call(
         functools.partial(dispatch_kernel, *sizes),
-        out_shape=[jax.ShapeDtypeStruct(tok.shape, tok.dtype)] * 2,
-        in_specs=[vmem] * 2,
-        out_specs=[vmem] * 2,
+        out_shape=[
+            *[jax.ShapeDtypeStruct(tok.shape, tok.dtype)] * 2,
+            *[jax.ShapeDtypeStruct((wg.shape[0], tok.shape[0]), jnp.float32)] * 2,
+            jax.ShapeDtypeStruct((wg.shape[0], tok.shape[0]), jnp.bfloat16),
+            jax.ShapeDtypeStruct(tok.shape, jnp.bfloat16),
+        ],
+        in_specs=[vmem] * 2 + [pl.BlockSpec(memory_space=pl.ANY)] * 3,
+        out_specs=[vmem] * 6,
         scratch_shapes=[
+            *[pltpu.VMEM(wg.shape, wg.dtype)] * 3,
+            dma((3,)),
             dma((2,)),
             *pair(units), *pair(units, max(1, nx - 1)), *pair(units, max(1, ny - 1)),
             *pair(units, diag), *pair(units, diag), *pair(units, chips),
         ],
-        compiler_params=pltpu.CompilerParams(collective_id=0, has_side_effects=True),
-    )(tok, grad)
+        compiler_params=pltpu.CompilerParams(
+            collective_id=0, has_side_effects=True, vmem_limit_bytes=56 * 1024 * 1024
+        ),
+    )(tok, grad, wg, wu, wd)
 
 
 def combine_kernel(
-    ny, nz, nx, cap, width, part, sq, ret, sq_out,
-    pair, out_buf, in_buf, acc, summed, sq_own, sq_in,
+    ny, nz, nx, cap, width, part, rows, grads, gate_t, up_t, hid_t, wd,
+    ret, sq_out, dgate_t, dup_t, gh, wd_v, w_sem, pair, out_buf, in_buf, acc, summed, sq_own, sq_in,
     ps, pr, cs, cr, zs, zr, ss, sr,
 ):
     here = Place(ny, nz, nx, width)
     for_diag = [(k, i) for k in range(1, ny) for i in range(1, nx)]
+    load = pltpu.make_async_copy(wd, wd_v, w_sem)
+    load.start()
     here.enter([here.at(k, 0, i) for k, i in for_diag])
     order = for_diag + [(0, i) for i in range(1, nx)] + [(k, 0) for k in range(1, ny)] + [(0, 0)]
     pending = []
@@ -232,8 +288,6 @@
         sq_own[level + 1] = total
         return base + len(peers)
 
-    sq_own[0] = sq[...]
-    base = stage(0, [(partner, 0)], 0)
     for k, i in order:
         o = k * nx + i
         swaps[o].wait_recv()
@@ -245,6 +299,17 @@
             started(
                 remote(out_buf.at[o], in_buf.at[o], cs.at[o], cr.at[o], here.at(k, 0, i))
             )
+    load.wait()
+    against_slots(wd_v, grads, gh)
+    activated, derivative = silu_parts(gate_t[...])
+    dgate_t[...] = (gh[...] * up_t[...] * derivative).astype(jnp.bfloat16)
+    dup_t[...] = (gh[...] * activated).astype(jnp.bfloat16)
+    delta_gram = against_rows(dgate_t[...], dgate_t[...]) + against_rows(dup_t[...], dup_t[...])
+    square = delta_gram * across_width(rows[...], rows[...])
+    hidden_gram = against_rows(hid_t[...], hid_t[...])
+    square = jnp.sum(square + hidden_gram * across_width(grads[...], grads[...]))
+    sq_own[0] = jnp.full((8, 128), square, jnp.float32)
+    base = stage(0, [(partner, 0)], 0)
     base = stage(1, [(here.at(dz=j), 0) for j in range(1, nz)], base)
     base = stage(2, [(here.at(dx=i), 0) for i in range(1, nx)], base)
     base = stage(3, [(here.at(dy=k), 0) for k in range(1, ny)], base)
@@ -276,23 +341,29 @@
         copy.wait_send()
 
 
-def combine(sizes, part, square):
+def combine(sizes, part, *rest):
     ny, nz, nx, cap, width = sizes
     slots, chips = nz * cap, nx * ny
     peers = 1 + (nz - 1) + (nx - 1) + (ny - 1)
     dma = pltpu.SemaphoreType.DMA
     twice = lambda count: [dma((count,)), dma((count,))]
     vmem = pl.BlockSpec(memory_space=pltpu.VMEM)
-    flat = jnp.full((8, 128), square, jnp.float32)
+    hid = rest[-1].shape
+    slot_hid = jax.ShapeDtypeStruct((hid[0], slots), jnp.bfloat16)
     return pl.pallas_call(
         functools.partial(combine_kernel, *sizes),
         out_shape=[
             jax.ShapeDtypeStruct((slots, width), jnp.bfloat16),
             jax.ShapeDtypeStruct((8, 128), jnp.float32),
+            slot_hid,
+            slot_hid,
         ],
-        in_specs=[vmem] * 2,
-        out_specs=[vmem] * 2,
+        in_specs=[vmem] * 6 + [pl.BlockSpec(memory_space=pl.ANY)],
+        out_specs=[vmem] * 4,
         scratch_shapes=[
+            pltpu.VMEM((hid[0], slots), jnp.float32),
+            pltpu.VMEM(hid, jnp.bfloat16),
+            dma(()),
             *[pltpu.VMEM((chips, slots, width), jnp.bfloat16)] * 3,
             pltpu.VMEM((slots, width), jnp.float32),
             pltpu.VMEM((slots, width), jnp.bfloat16),
@@ -303,7 +374,7 @@
         compiler_params=pltpu.CompilerParams(
             collective_id=1, has_side_effects=True, vmem_limit_bytes=48 * 1024 * 1024
         ),
-    )(part, flat)
+    )(part, *rest)
 
 
 def on_device(sizes, count, tokens, expert_ids, route_weight, cotangent, w_gate, w_up, w_down):
@@ -328,21 +399,13 @@
         axis=1,
     )
     grad_slots = (slot_weight[:, None] * picked_cot).astype(jnp.bfloat16)
-    slot_rows, slot_grads = dispatch(sizes, token_slots, grad_slots)
-    gate_weight, up_weight, down_weight = w_gate[0], w_up[0], w_down[0]
-    pre_gate = across_width(slot_rows, gate_weight)
-    pre_up = across_width(slot_rows, up_weight)
-    activated, derivative = silu_parts(pre_gate)
-    hidden = (activated * pre_up).astype(jnp.bfloat16)
-    partial_value = jnp.dot(hidden, down_weight, preferred_element_type=jnp.float32)
-    grad_hidden = across_width(slot_grads, down_weight)
-    delta_gate = (grad_hidden * pre_up * derivative).astype(jnp.bfloat16)
-    delta_up = (grad_hidden * activated).astype(jnp.bfloat16)
-    gram_rows = across_width(slot_rows, slot_rows)
-    gram_grads = across_width(slot_grads, slot_grads)
-    gram_delta = across_width(delta_gate, delta_gate) + across_width(delta_up, delta_up)
-    square = jnp.sum(gram_rows * gram_delta) + jnp.sum(gram_grads * across_width(hidden, hidden))
-    returned_rows, square_all = combine(sizes, partial_value.astype(jnp.bfloat16), square)
+    down_weight = w_down[0]
+    slot_rows, slot_grads, gate_t, up_t, hid_t, part = dispatch(
+        sizes, token_slots, grad_slots, w_gate[0], w_up[0], down_weight
+    )
+    returned_rows, square_all, dgate_t, dup_t = combine(
+        sizes, part, slot_rows, slot_grads, gate_t, up_t, hid_t, down_weight
+    )
     weight_hot = [h.astype(jnp.bfloat16) for h in hot]
     picked = [against_rows(h, returned_rows) for h in weight_hot]
     layer_out = (route_weight[:, 0:1] * picked[0] + route_weight[:, 1:2] * picked[1]).astype(
@@ -351,9 +414,9 @@
     inv_rms = lax.rsqrt(jnp.maximum(square_all[0, 0], 0.0) / count + 1e-06)
     return (
         layer_out,
-        (against_rows(delta_gate, slot_rows) * inv_rms).astype(jnp.bfloat16)[None],
-        (against_rows(delta_up, slot_rows) * inv_rms).astype(jnp.bfloat16)[None],
-        (against_rows(hidden, slot_grads) * inv_rms).astype(jnp.bfloat16)[None],
+        (along(dgate_t, slot_rows) * inv_rms).astype(jnp.bfloat16)[None],
+        (along(dup_t, slot_rows) * inv_rms).astype(jnp.bfloat16)[None],
+        (along(hid_t, slot_grads) * inv_rms).astype(jnp.bfloat16)[None],
     )
 
 

time: 114 us -> 102 us (0.89)
  matrix products: 43.4 us -> 21.9 us
  Pallas kernels: 63.8 us -> 69.6 us
  local copies, waits for them, and re-layouts: 1.48 us -> 6.25 us
  between operations: 2.87 us -> 1.38 us
    dot_general x5 -> x2, matrix products: 16.8 us -> 1.12 us  [against_rows(): lax.dot_general(left_rows, right_rows, (((0,), (0,)), ((), ())), preferre...]
    dot_general x9 -> x3, matrix products: 22.5 us -> 15.4 us  [along(): return jnp.dot(left, right, preferred_element_type=jnp.float32)]
    pallas_call x1, Pallas kernels: 34.5 us -> 39.9 us  [dispatch(): pl.pallas_call(functools.partial(dispatch_kernel, *sizes), out_shape=[*[j...]
    unnamed x30 -> x14, local copies, waits for them, and re-layouts: 0.2 us -> 4.98 us
    dot_general x1, matrix products: 2.01 us -> 3.23 us  [on_device(): jnp.dot(hot_any, tokens, preferred_element_type=jnp.float32)]
where the time goes in v2:
time: 102 us; the launch traced here: 101 us
  Pallas kernels  69.6 us (68%)
  matrix products  21.9 us (21%)
  local copies, waits for them, and re-layouts  6.25 us (6%)
  other arithmetic  2.29 us (2%)
  between operations  1.38 us (1%)
    pallas_call x1, Pallas kernels, dispatch(): pl.pallas_call(functools.partial(dispatch_kernel, *sizes), out_shape=[*[j...  39.9 us
    pallas_call x1, Pallas kernels, combine(): pl.pallas_call(functools.partial(combine_kernel, *sizes), out_shape=[jax....  29.7 us
    dot_general x3, matrix products, along(): return jnp.dot(left, right, preferred_element_type=jnp.float32)  15.4 us
    unnamed x14, local copies, waits for them, and re-layouts  4.98 us
    dot_general x1, matrix products, on_device(): jnp.dot(hot_any, tokens, preferred_element_type=jnp.float32)  3.23 us

profile of v2, /device:TPU:0, one launch (start us, length us, event | category | flops | bytes accessed | tf_op | source)
XLA Modules:
  0.0 101.4 jit_solution(5990477382540731972)
XLA Ops:
  0.6 0.0 copy-start
  0.6 0.8 fusion.16
  1.4 0.1 convolution_convert_fusion.1
  1.6 0.7 select_reduce_fusion
  2.3 0.7 multiply_add_fusion
  3.0 0.8 slice_bitcast_fusion.3
  3.7 0.1 add_reduce_fusion
  3.8 0.0 copy-done
  3.9 2.0 %fusion.3.grad = bf16[256,4096]{1,0:T(8,128)(2,1)} fusion(bf16[128,4096]{1,0:T(8,128)(2,1)S(1)} %copy-done, f32[256]{0:T(256)S(1)} %add_reduce_fusion, s32[128]{0:T(128)S(1)} %get-tuple-element.27, s32[128]{0:T(128)S(1)} %get-tuple-element.26), kind=kOutput, calls=%fused_computation.8 | convolution fusion | flops 270630912 | bytes 3147776 | tf_op jit(solution)/shard_map/dot_general | solution.py:395
  5.9 3.2 %convolution_convert_fusion.tok = bf16[256,4096]{1,0:T(8,128)(2,1)} fusion(bf16[128,4096]{1,0:T(8,128)(2,1)} %param.7, s32[128]{0:T(128)S(1)} %get-tuple-element.27, s32[128]{0:T(128)S(1)} %get-tuple-element.26), kind=kOutput, calls=%fused_computation.7 | convolution fusion | flops 269582336 | bytes 3146752 | tf_op jit(solution)/shard_map/dot_general | solution.py:394
  9.1 39.9 %shard_map.102 = (bf16[256,4096]{1,0:T(8,128)(2,1)}, bf16[256,4096]{1,0:T(8,128)(2,1)}, f32[896,256]{1,0:T(8,128)}, f32[896,256]{1,0:T(8,128)}, bf16[896,256]{1,0:T(8,128)(2,1)}, /*index=5*/bf16[256,4096]{1,0:T(8,128)(2,1)}) custom-call(bf16[256,4096]{1,0:T(8,128)(2,1)} %convolution_convert_fusion.tok, bf16[256,4096]{1,0:T(8,128)(2,1)} %fusion.3.grad, ...), custom_call_target="tpu_custom_call" | custom-call | tf_op jit(solution)/shard_map/pallas_call | solution.py:228
  49.0 0.0 copy-start.1
  49.0 1.0 copy-done.1
  50.1 0.0 copy-start.2
  50.1 1.6 %copy-done.2 = bf16[256,4096]{1,0:T(8,128)(2,1)S(1)} copy-done((bf16[256,4096]{1,0:T(8,128)(2,1)S(1)}, bf16[256,4096]{1,0:T(8,128)(2,1)}, u32[]{:S(2)}) %copy-start.2) | copy-done | bytes 2097176
  51.6 0.0 copy-start.3
  51.6 1.2 %copy-done.3 = f32[896,256]{1,0:T(8,128)S(1)} copy-done((f32[896,256]{1,0:T(8,128)S(1)}, f32[896,256]{1,0:T(8,128)}, u32[]{:S(2)}) %copy-start.3) | copy-done | bytes 917528
  52.8 0.0 copy-start.4
  52.8 1.2 %copy-done.4 = f32[896,256]{1,0:T(8,128)S(1)} copy-done((f32[896,256]{1,0:T(8,128)S(1)}, f32[896,256]{1,0:T(8,128)}, u32[]{:S(2)}) %copy-start.4) | copy-done | bytes 917528
  54.0 0.0 copy-start.6
  54.0 29.7 %shard_map.103 = (bf16[256,512]{1,0:T(8,128)(2,1)S(1)}, f32[8,128]{1,0:T(8,128)S(1)}, bf16[896,256]{1,0:T(8,128)(2,1)S(1)}, bf16[896,256]{1,0:T(8,128)(2,1)S(1)}) custom-call(bf16[256,4096]{1,0:T(8,128)(2,1)S(1)} %copy-done.2, bf16[256,4096]{1,0:T(8,128)(2,1)} %get-tuple-element.15.rows, bf16[256,4096]{1,0:T(8,128)(2,1)} %get-tuple-element.16.grads, ...), custom_call_target="tpu_custom_call" | custom-call | tf_op jit(solution)/shard_map/pallas_call | solution.py:353
  83.7 0.5 slice.21
  84.9 0.2 convolution_multiply_fusion.2
  85.1 0.9 fusion.5
  86.0 0.0 copy-done.6
  86.0 0.0 copy-start.5
  86.0 5.1 %fusion.2 = bf16[1,896,4096]{2,1,0:T(8,128)(2,1)} fusion(f32[]{:T(128)} %bitcast.7, bf16[896,256]{1,0:T(8,128)(2,1)S(1)} %copy-done.1, bf16[256,4096]{1,0:T(8,128)(2,1)S(1)} %copy-done.6), kind=kOutput, calls=%fused_computation.5 | convolution fusion | flops 1886388224 | bytes 9895940 | tf_op jit(solution)/shard_map/dot_general | solution.py:31
  91.2 0.0 copy-done.5
  91.2 5.1 %fusion = bf16[1,896,4096]{2,1,0:T(8,128)(2,1)} fusion(f32[]{:T(128)} %bitcast.7, bf16[896,256]{1,0:T(8,128)(2,1)S(1)} %get-tuple-element.21, bf16[256,4096]{1,0:T(8,128)(2,1)S(1)} %copy-done.5), kind=kOutput, calls=%fused_computation.3 | convolution fusion | flops 1886388224 | bytes 9895940 | tf_op jit(solution)/shard_map/dot_general | solution.py:31
  96.3 5.1 %fusion.1 = bf16[1,896,4096]{2,1,0:T(8,128)(2,1)} fusion(f32[]{:T(128)} %bitcast.7, bf16[896,256]{1,0:T(8,128)(2,1)S(1)} %get-tuple-element.23, bf16[256,4096]{1,0:T(8,128)(2,1)S(1)} %copy-done.5), kind=kOutput, calls=%fused_computation.4 | convolution fusion | flops 1886388224 | bytes 9895940 | tf_op jit(solution)/shard_map/dot_general | solution.py:31
  (1 shorter events, 0.0 us)
Async XLA Ops:
  0.6 3.2 %copy-start = (bf16[128,4096]{1,0:T(8,128)(2,1)S(1)}, bf16[128,4096]{1,0:T(8,128)(2,1)}, u32[]{:S(2)}) copy-start(bf16[128,4096]{1,0:T(8,128)(2,1)} %param.10) | copy-start | bytes 3145732
  49.0 1.0 %copy-start.1 = (bf16[896,256]{1,0:T(8,128)(2,1)S(1)}, bf16[896,256]{1,0:T(8,128)(2,1)}, u32[]{:S(2)}) copy-start(bf16[896,256]{1,0:T(8,128)(2,1)} %get-tuple-element.19.hid_t) | copy-start | bytes 1376260
  50.1 1.6 %copy-start.2 = (bf16[256,4096]{1,0:T(8,128)(2,1)S(1)}, bf16[256,4096]{1,0:T(8,128)(2,1)}, u32[]{:S(2)}) copy-start(bf16[256,4096]{1,0:T(8,128)(2,1)} %get-tuple-element.14.part) | copy-start | bytes 6291460
  51.6 1.2 %copy-start.3 = (f32[896,256]{1,0:T(8,128)S(1)}, f32[896,256]{1,0:T(8,128)}, u32[]{:S(2)}) copy-start(f32[896,256]{1,0:T(8,128)} %get-tuple-element.17.gate_t) | copy-start | bytes 2752516
  52.8 1.2 %copy-start.4 = (f32[896,256]{1,0:T(8,128)S(1)}, f32[896,256]{1,0:T(8,128)}, u32[]{:S(2)}) copy-start(f32[896,256]{1,0:T(8,128)} %get-tuple-element.18.up_t) | copy-start | bytes 2752516
  54.0 32.0 %copy-start.6 = (bf16[256,4096]{1,0:T(8,128)(2,1)S(1)}, bf16[256,4096]{1,0:T(8,128)(2,1)}, u32[]{:S(2)}) copy-start(bf16[256,4096]{1,0:T(8,128)(2,1)} %get-tuple-element.16.grads) | copy-start | bytes 6291460
  86.0 5.1 %copy-start.5 = (bf16[256,4096]{1,0:T(8,128)(2,1)S(1)}, bf16[256,4096]{1,0:T(8,128)(2,1)}, u32[]{:S(2)}) copy-start(bf16[256,4096]{1,0:T(8,128)(2,1)} %get-tuple-element.15.rows) | copy-start | bytes 6291460
